TPU v7x, 32 devices: a whole 2x2x4 slice. The times are simulated.
32 devices in a mesh: dp: 16 (over z, y, core), tensor: 2 (over x).
Axes of the slice: x: 2, y: 2, z: 4, core: 2. Of those that a mesh axis runs over, the one named last changes fastest.
Arguments:
- layer_input: bfloat16 [16384, 1024], P(('dp', 'tensor')), may hold values from -6 to 6
- segments: int32 [16384], P('dp'), may hold values from 0 to 127, never falling along the last dimension, each value on 1 to 256 neighbouring positions
- w_qkv: bfloat16 [1024, 3, 1024], P(None, None, 'tensor'), may hold values from -0.1875 to 0.1875
- w_out: bfloat16 [1024, 1024], P('tensor'), may hold values from -2 to 2
- w_up: bfloat16 [1024, 4096], P(None, 'tensor'), may hold values from -0.1875 to 0.1875
- w_down: bfloat16 [4096, 1024], P('tensor'), may hold values from -0.09375 to 0.09375
- norm1_gain: float32 [1024], replicated, may hold values from 0.5 to 1.5
- norm1_bias: float32 [1024], replicated, may hold values from -3 to 3
- norm2_gain: float32 [1024], replicated, may hold values from 0.5 to 1.5
- norm2_bias: float32 [1024], replicated, may hold values from -3 to 3
- out_grad: bfloat16 [16384, 1024], P(('dp', 'tensor')), may hold values from -6 to 6
Outputs:
- output: bfloat16 [16384, 1024], P(('dp', 'tensor'))
- input_grad: bfloat16 [16384, 1024], P(('dp', 'tensor'))
- grad_qkv: float32 [1024, 3, 1024], P(None, None, 'tensor')
- grad_out: float32 [1024, 1024], P('tensor')
- grad_up: float32 [1024, 4096], P(None, 'tensor')
- grad_down: float32 [4096, 1024], P('tensor')
- grad_gain1: float32 [1024], replicated
- grad_bias1: float32 [1024], replicated
- grad_gain2: float32 [1024], replicated
- grad_bias2: float32 [1024], replicated
Inputs may be any that keep to these rules, and one draw needn't show every extreme that they name: `segments`: segment ids never fall along the tokens; each protein has 1 to 256 tokens and attends only within its packed row of 512.
All inputs are finite; a program needn't handle non-finite values.
Results may differ from a plain program's by a relative error of at most 0.02.
Values may be sent and summed in bfloat16 or wider, within the bound.
A program may use at most 192 MiB of HBM per device.

v0:
```python
import jax
import jax.numpy as jnp
from jax import lax
from jax.sharding import PartitionSpec as P

HEAD_DIM = 64
ROW_LEN = 512
EPS = 1e-12
NEG_LARGE = -1e30
SQRT_HALF = 0.7071067811865476
INV_ROOT_TWO_PI = 0.3989422804014327


def gelu_exact(values):
    return 0.5 * values * (1.0 + lax.erf(values * SQRT_HALF))


def gelu_slope(values):
    return (
        0.5 * (1.0 + lax.erf(values * SQRT_HALF))
        + values * jnp.exp(-0.5 * values * values) * INV_ROOT_TWO_PI
    )


def layer_norm(values, gain, bias):
    average = jnp.mean(values, axis=-1, keepdims=True)
    centred = values - average
    inverse = lax.rsqrt(jnp.mean(centred * centred, axis=-1, keepdims=True) + EPS)
    normed = centred * inverse
    return (normed * gain + bias, normed, inverse)


def norm_back(grad, normed, inverse, gain):
    scaled = grad * gain
    return inverse * (
        scaled
        - jnp.mean(scaled, axis=-1, keepdims=True)
        - normed * jnp.mean(scaled * normed, axis=-1, keepdims=True)
    )


def masked_scores(queries, keys, row_segments, factor):
    scores = jnp.einsum("qhd,khd->hqk", queries, keys, preferred_element_type=jnp.float32) * factor
    same = row_segments[:, None] == row_segments[None, :]
    return jnp.where(same[None], scores, NEG_LARGE)


def contract_rows(left, right):
    return lax.dot_general(
        left, right, (((0,), (0,)), ((), ())), preferred_element_type=jnp.float32
    )


def contract_cols(left, right):
    return lax.dot_general(
        left, right, (((1,), (1,)), ((), ())), preferred_element_type=jnp.float32
    )


def body(
    layer_input,
    segments,
    w_qkv,
    w_out,
    w_up,
    w_down,
    norm1_gain,
    norm1_bias,
    norm2_gain,
    norm2_bias,
    out_grad,
):
    head_width = HEAD_DIM
    row_length = ROW_LEN
    factor = head_width ** (-0.5)
    qkv_use, out_use = (w_qkv, w_out)
    source = lax.all_gather(layer_input, "tensor", axis=0, tiled=True)
    local_width = qkv_use.shape[2]
    local_heads = local_width // head_width
    group_rows = source.shape[0]
    blocks = group_rows // row_length
    joined = jnp.einsum("td,dsc->tsc", source, qkv_use, preferred_element_type=jnp.float32).astype(
        jnp.bfloat16
    )
    joined_blocks = joined.reshape(blocks, row_length, 3, local_heads, head_width)
    segment_blocks = segments.reshape(blocks, row_length)

    def attend(pack):
        block, row_segments = pack
        scores = masked_scores(block[:, 0], block[:, 1], row_segments, factor)
        top = jnp.max(scores, axis=-1, keepdims=True)
        expo = jnp.exp(scores - top)
        total = jnp.sum(expo, axis=-1, keepdims=True)
        probs = (expo / total).astype(jnp.bfloat16)
        mixed = jnp.einsum("hqk,khd->qhd", probs, block[:, 2], preferred_element_type=jnp.float32)
        return (
            mixed.reshape(row_length, local_width).astype(jnp.bfloat16),
            (top + jnp.log(total))[..., 0],
        )

    attended, log_totals = lax.map(attend, (joined_blocks, segment_blocks))
    attended = attended.reshape(group_rows, local_width)
    attn_out = lax.psum_scatter(
        jnp.dot(attended, out_use, preferred_element_type=jnp.float32).astype(jnp.bfloat16),
        "tensor",
        scatter_dimension=0,
        tiled=True,
    ).astype(jnp.float32)
    hidden, normed_one, inverse_one = layer_norm(
        layer_input.astype(jnp.float32) + attn_out, norm1_gain, norm1_bias
    )
    hidden_low = hidden.astype(jnp.bfloat16)
    hidden_group = lax.all_gather(hidden_low, "tensor", axis=0, tiled=True)
    upper = jnp.dot(hidden_group, w_up, preferred_element_type=jnp.float32)
    active = gelu_exact(upper).astype(jnp.bfloat16)
    ffn_out = lax.psum_scatter(
        jnp.dot(active, w_down, preferred_element_type=jnp.float32).astype(jnp.bfloat16),
        "tensor",
        scatter_dimension=0,
        tiled=True,
    ).astype(jnp.float32)
    result, normed_two, inverse_two = layer_norm(hidden + ffn_out, norm2_gain, norm2_bias)
    grad_result = out_grad.astype(jnp.float32)
    grad_gain2 = jnp.sum(grad_result * normed_two, axis=0)
    grad_bias2 = jnp.sum(grad_result, axis=0)
    grad_second = norm_back(grad_result, normed_two, inverse_two, norm2_gain)
    branch_low = grad_second.astype(jnp.bfloat16)
    branch_group = lax.all_gather(branch_low, "tensor", axis=0, tiled=True)
    grad_active = contract_cols(branch_group, w_down)
    grad_upper = (grad_active * gelu_slope(upper)).astype(jnp.bfloat16)
    grad_down = contract_rows(active, branch_group)
    grad_up = contract_rows(hidden_group, grad_upper)
    hidden_part = lax.psum_scatter(
        contract_cols(grad_upper, w_up).astype(jnp.bfloat16),
        "tensor",
        scatter_dimension=0,
        tiled=True,
    ).astype(jnp.float32)
    grad_hidden = grad_second + hidden_part
    grad_gain1 = jnp.sum(grad_hidden * normed_one, axis=0)
    grad_bias1 = jnp.sum(grad_hidden, axis=0)
    grad_first = norm_back(grad_hidden, normed_one, inverse_one, norm1_gain)
    attn_low = grad_first.astype(jnp.bfloat16)
    attn_group = lax.all_gather(attn_low, "tensor", axis=0, tiled=True)
    grad_mixed = contract_cols(attn_group, out_use).astype(jnp.bfloat16)
    grad_out_w = contract_rows(attended, attn_group)
    grad_mixed_blocks = grad_mixed.reshape(blocks, row_length, local_heads, head_width)

    def attend_back(pack):
        block, row_segments, log_total, grad_block = pack
        queries = block[:, 0]
        keys = block[:, 1]
        values = block[:, 2]
        scores = masked_scores(queries, keys, row_segments, factor)
        probs = jnp.exp(scores - log_total[..., None])
        grad_probs = jnp.einsum(
            "qhd,khd->hqk", grad_block, values, preferred_element_type=jnp.float32
        )
        grad_scores = probs * (grad_probs - jnp.sum(probs * grad_probs, axis=-1, keepdims=True))
        grad_scores = grad_scores.astype(jnp.bfloat16)
        grad_query = (
            jnp.einsum("hqk,khd->qhd", grad_scores, keys, preferred_element_type=jnp.float32)
            * factor
        )
        grad_key = (
            jnp.einsum("hqk,qhd->khd", grad_scores, queries, preferred_element_type=jnp.float32)
            * factor
        )
        grad_value = jnp.einsum(
            "hqk,qhd->khd",
            probs.astype(jnp.bfloat16),
            grad_block,
            preferred_element_type=jnp.float32,
        )
        stacked = jnp.stack([grad_query, grad_key, grad_value], axis=1)
        return stacked.reshape(row_length, 3, local_width).astype(jnp.bfloat16)

    grad_joined = lax.map(
        attend_back, (joined_blocks, segment_blocks, log_totals, grad_mixed_blocks)
    )
    grad_joined = grad_joined.reshape(group_rows, 3, local_width)
    grad_qkv_w = jnp.einsum("td,tsc->dsc", source, grad_joined, preferred_element_type=jnp.float32)
    input_part = lax.psum_scatter(
        jnp.einsum("tsc,dsc->td", grad_joined, qkv_use, preferred_element_type=jnp.float32).astype(
            jnp.bfloat16
        ),
        "tensor",
        scatter_dimension=0,
        tiled=True,
    ).astype(jnp.float32)
    grad_input = grad_first + input_part
    summed_qkv, summed_out, summed_up, summed_down = (
        lax.psum(grad_qkv_w.astype(jnp.bfloat16), "dp").astype(jnp.float32),
        lax.psum(grad_out_w.astype(jnp.bfloat16), "dp").astype(jnp.float32),
        lax.psum(grad_up.astype(jnp.bfloat16), "dp").astype(jnp.float32),
        lax.psum(grad_down.astype(jnp.bfloat16), "dp").astype(jnp.float32),
    )
    summed_gain1, summed_bias1, summed_gain2, summed_bias2 = lax.psum(
        (grad_gain1, grad_bias1, grad_gain2, grad_bias2), ("dp", "tensor")
    )
    return (
        result.astype(jnp.bfloat16),
        grad_input.astype(jnp.bfloat16),
        summed_qkv,
        summed_out,
        summed_up,
        summed_down,
        summed_gain1,
        summed_bias1,
        summed_gain2,
        summed_bias2,
    )


def solution(mesh):
    return jax.shard_map(
        body,
        mesh=mesh,
        in_specs=(
            P(("dp", "tensor"), None),
            P("dp"),
            P(None, None, "tensor"),
            P("tensor", None),
            P(None, "tensor"),
            P("tensor", None),
            P(),
            P(),
            P(),
            P(),
            P(("dp", "tensor"), None),
        ),
        out_specs=(
            P(("dp", "tensor"), None),
            P(("dp", "tensor"), None),
            P(None, None, "tensor"),
            P("tensor", None),
            P(None, "tensor"),
            P("tensor", None),
            P(),
            P(),
            P(),
            P(),
        ),
        check_vma=False,
    )
```

profile of v0, /device:TPU:0, one launch (start us, length us, event | category | flops | bytes accessed | tf_op | source)
XLA Modules:
  0.0 702.6 jit_solution(4263438143487047636)
XLA Ops:
  8.8 36.6 %all-gather.5.cloned.1.call-done = bf16[1024,1024]{1,0:T(8,128)(2,1)} async-done(((bf16[512,1024]{1,0:T(8,128)(2,1)}), bf16[1024,1024]{1,0:T(8,128)(2,1)}) %all-gather.5.cloned.1.call-update) | async-done | bytes 2097168 | tf_op jit(solution)/shard_map/all_gather | solution.py:77
  45.4 6.3 convolution_convert_fusion.2
  51.7 8.9 %reshape.242 = bf16[2,512,3,8,64]{4,3,1,0,2:T(8,128)(2,1)} reshape(bf16[1024,3,512]{2,0,1:T(8,128)(2,1)} %convolution_convert_fusion.2) | data formatting | bytes 6291456 | tf_op jit(solution)/shard_map/reshape | solution.py:85
  60.6 7.6 %copy.35 = bf16[2,512,3,8,64]{1,4,3,2,0:T(8,128)(2,1)} copy(bf16[2,512,3,8,64]{4,3,1,0,2:T(8,128)(2,1)} %reshape.242) | data formatting | bytes 6291456 | tf_op jit(solution)/shard_map/while | solution.py:101
  68.2 24.3 %while.22 = (s32[]{:T(128)}, bf16[2,512,512]{2,1,0:T(8,128)(2,1)}, f32[2,8,512]{2,1,0:T(8,128)S(1)}, bf16[2,512,3,8,64]{1,4,3,2,0:T(8,128)(2,1)}, s32[2,512]{1,0:T(2,128)S(1)}, /*index=5*/s32[]{:T(128)}) while((s32[]{:T(128)}, bf16[2,512,512]{2,1,0:T(8,128)(2,1)}, f32[2,8,512]{2,1,0:T(8,128)S(1)}, bf16[2,512,3,8,64]{1,4,3,2,0:T(8,128)(2,1)}, ...), condition=%wide.region_3.4_spmd, body=%wide.region_0.3_spmd.sunk | while | flops 562556928 | bytes 33692240 | solution.py:101
  68.5 1.5 dynamic-slice_bitcast_fusion.6
  70.0 1.5 fusion.85
  71.5 1.7 fusion.86
  73.2 3.2 fusion.87
  76.4 2.0 copy.58
  78.5 1.9 constant_dynamic-update-slice_fusion.4
  80.6 1.5 dynamic-slice_bitcast_fusion.6
  82.1 1.5 fusion.85
  83.6 1.7 fusion.86
  85.4 3.2 fusion.87
  88.6 2.0 copy.58
  90.6 1.9 constant_dynamic-update-slice_fusion.4
  92.5 4.1 convolution_convert_fusion.5
  96.7 32.0 %reduce-scatter.5.cloned.1.call-done = bf16[512,1024]{1,0:T(8,128)(2,1)} async-done(((bf16[1024,1024]{1,0:T(8,128)(2,1)}), bf16[512,1024]{1,0:T(8,128)(2,1)}) %reduce-scatter.5.cloned.1.call-update) | async-done | bytes 1048592 | tf_op jit(solution)/shard_map/reduce_scatter | solution.py:103
  128.7 2.0 fusion.42
  130.7 2.0 multiply_reduce_fusion.4
  132.8 1.5 fusion.44
  134.6 33.0 %all-gather.7.cloned.1.call-done = bf16[1024,1024]{1,0:T(8,128)(2,1)} async-done(((bf16[512,1024]{1,0:T(8,128)(2,1)}), bf16[1024,1024]{1,0:T(8,128)(2,1)}) %all-gather.7.cloned.1.call-update) | async-done | bytes 2097168 | tf_op jit(solution)/shard_map/all_gather | solution.py:113
  167.6 9.5 %multiply_convert_fusion.1 = (bf16[1024,2048]{1,0:T(8,128)(2,1)S(1)}, f32[1024,2048]{1,0:T(8,128)}) fusion(bf16[1024,1024]{1,0:T(8,128)(2,1)} %all-gather.7.cloned.1.call-done, bf16[1024,2048]{1,0:T(8,128)(2,1)} %param.19), kind=kOutput, calls=%fused_computation.55 | convolution fusion | flops 4305453056 | bytes 18874368 | tf_op jit(solution)/shard_map/dot_general | solution.py:114
  177.1 2.0 copy-done.27
  179.1 5.6 convolution_convert_fusion.4
  184.8 32.0 %reduce-scatter.7.cloned.1.call-done = bf16[512,1024]{1,0:T(8,128)(2,1)} async-done(((bf16[1024,1024]{1,0:T(8,128)(2,1)}), bf16[512,1024]{1,0:T(8,128)(2,1)}) %reduce-scatter.7.cloned.1.call-update) | async-done | bytes 1048592 | tf_op jit(solution)/shard_map/reduce_scatter | solution.py:116
  216.8 2.8 fusion.49
  220.0 1.6 fusion.38
  221.6 2.9 fusion.47
  224.7 33.0 %all-gather.9.cloned.1.call-done = bf16[1024,1024]{1,0:T(8,128)(2,1)} async-done(((bf16[512,1024]{1,0:T(8,128)(2,1)}), bf16[1024,1024]{1,0:T(8,128)(2,1)}) %all-gather.9.cloned.1.call-update) | async-done | bytes 2097168 | tf_op jit(solution)/shard_map/all_gather | solution.py:128
  257.7 10.3 %fusion.31 = bf16[1024,2048]{1,0:T(8,128)(2,1)S(1)} fusion(f32[1024,2048]{1,0:T(8,128)} %get-tuple-element.165, bf16[1024,1024]{1,0:T(8,128)(2,1)} %all-gather.9.cloned.1.call-done, bf16[2048,1024]{1,0:T(8,128)(2,1)} %param.20), kind=kOutput, calls=%fused_computation.54 | convolution fusion | flops 4315938816 | bytes 18874368 | tf_op jit(solution)/shard_map/dot_general | solution.py:55
  268.0 2.0 copy-done.25
  270.0 5.7 convolution_convert_fusion.3
  275.8 32.0 %reduce-scatter.9.cloned.1.call-done = bf16[512,1024]{1,0:T(8,128)(2,1)} async-done(((bf16[1024,1024]{1,0:T(8,128)(2,1)}), bf16[512,1024]{1,0:T(8,128)(2,1)}) %reduce-scatter.9.cloned.1.call-update) | async-done | bytes 1048592 | tf_op jit(solution)/shard_map/reduce_scatter | solution.py:133
  307.8 4.4 multiply_reduce_fusion.1
  312.3 2.5 fusion.46
  314.9 33.2 %all-gather.11.cloned.1.call-done = bf16[1024,1024]{1,0:T(8,128)(2,1)} async-done(((bf16[512,1024]{1,0:T(8,128)(2,1)}), bf16[1024,1024]{1,0:T(8,128)(2,1)}) %all-gather.11.cloned.1.call-update) | async-done | bytes 2097168 | tf_op jit(solution)/shard_map/all_gather | solution.py:144
  348.1 4.1 convolution_convert_fusion.7
  352.2 4.3 reshape.241
  356.5 3.3 copy.39
  359.8 39.5 %while.23 = (s32[]{:T(128)}, bf16[2,512,3,512]{3,1,0,2:T(8,128)(2,1)}, bf16[2,512,3,8,64]{1,4,3,2,0:T(8,128)(2,1)}, s32[2,512]{1,0:T(2,128)S(1)}, f32[2,8,512]{2...) while((s32[]{:T(128)}, bf16[2,512,3,512]{3,1,0,2:T(8,128)(2,1)}, ...), condition=%wide.region_17.18_spmd, body=%wide.region_15.17_spmd.sunk | while | flops 1376776192 | bytes 86104704 | solution.py:178
  362.9 2.9 multiply_reduce_fusion.7
  365.8 2.7 multiply_convert_fusion.3
  370.7 2.3 fusion.93
  374.3 2.6 copy.59
  376.9 2.7 constant_dynamic-update-slice_fusion.5
  382.7 2.9 multiply_reduce_fusion.7
  385.6 2.7 multiply_convert_fusion.3
  390.4 2.3 fusion.93
  394.0 2.6 copy.59
  396.6 2.7 constant_dynamic-update-slice_fusion.5
  399.3 6.6 bitcast_convert_fusion
  406.1 9.6 %convolution_convert_fusion = bf16[2048,1024]{1,0:T(8,128)(2,1)} fusion(bf16[1024,2048]{1,0:T(8,128)(2,1)} %copy-done.27, bf16[1024,1024]{1,0:T(8,128)(2,1)} %all-gather.9.cloned.1.call-done), kind=kOutput, calls=%fused_computation.58 | convolution fusion | flops 4297064448 | bytes 10485760 | tf_op jit(solution)/shard_map/dot_general | solution.py:49
  415.7 6.2 convolution_convert_fusion.1
  422.0 2.3 convolution_convert_fusion.6
  424.3 4.9 convert_bitcast_fusion
  429.9 40.7 %all-reduce = (f32[1024]{0:T(1024)}, f32[1024]{0:T(1024)}, f32[1024]{0:T(1024)}, f32[1024]{0:T(1024)}) all-reduce(f32[1024]{0:T(1024)S(1)} %copy-done.17, f32[1024]{0:T(1024)S(1)} %copy-done.18, f32[1024]{0:T(1024)S(1)} %copy-done.14, f32[1024]{0:T(1024)S(1)} %copy-done.15), channel_id=1, replica_groups=mesh['dp'=16,'tensor'=2] {'dp','tensor'}, use_global_device_ids=true, to_apply=%region_24.25 | all-reduce | flops 4096 | bytes 32768 | tf_op jit(solution)/shard_map/psum | solution.py:198
  470.5 3.2 add_convert_fusion
  473.7 202.7 %all-reduce.4.cloned.1.call-done = (bf16[1024,3,512]{0,2,1:T(8,128)(2,1)}, bf16[512,1024]{1,0:T(8,128)(2,1)}, bf16[1024,2048]{1,0:T(8,128)(2,1)}, bf16[2048,1024]{1,0:T(8,128)(2,1)}) async-done(((bf16[1024,3,512]{0,2,1:T(8,128)(2,1)}, bf16[512,1024]{1,0:T(8,128)(2,1)}, bf16[1024,2048]{1,0:T(8,128)(2,1)}, bf16[2048,1024]{1,0:T(8,128)(2,1)}), (bf16[1024,3,512]{0,2,1:T(8,128)(2,1)}, ...) | async-done | bytes 12582928 | tf_op jit(solution)/shard_map/psum | solution.py:193
  676.4 6.8 convert_element_type.142
  683.2 4.4 convert_element_type.144
  687.7 5.4 copy.42
  693.1 2.8 convert_element_type.140
  (109 shorter events, 17.3 us)
Async XLA Ops:
  7.2 38.2 %copy-start = (bf16[1024,3,512]{2,0,1:T(8,128)(2,1)S(1)}, bf16[1024,3,512]{2,0,1:T(8,128)(2,1)}, u32[]{:S(2)}) copy-start(bf16[1024,3,512]{2,0,1:T(8,128)(2,1)} %param.17) | copy-start | bytes 9437188
  7.2 38.2 %all-gather.5.cloned.1.call-start = ((), (), s32[]{:S(2)}) async-start(), calls=%async_computation.4 | async-start | bytes 3145728 | tf_op jit(solution)/shard_map/all_gather | solution.py:77
  7.9 120.8 %reduce-scatter.5.cloned.1.call-start = ((), (), s32[]{:S(2)}) async-start(), calls=%async_computation.5 | async-start | bytes 3145728 | tf_op jit(solution)/shard_map/reduce_scatter | solution.py:103
  96.6 36.2 %copy-start.12 = (f32[1024]{0:T(1024)S(1)}, f32[1024]{0:T(1024)}, u32[]{:S(2)}) copy-start(f32[1024]{0:T(1024)} %param.21) | copy-start | bytes 12292
  96.6 36.2 %copy-start.16 = (f32[1024]{0:T(1024)S(1)}, f32[1024]{0:T(1024)}, u32[]{:S(2)}) copy-start(f32[1024]{0:T(1024)} %param.22) | copy-start | bytes 12292
  96.6 71.0 %all-gather.7.cloned.1.call-start = ((), (), s32[]{:S(2)}) async-start(), calls=%async_computation.6 | async-start | bytes 3145728 | tf_op jit(solution)/shard_map/all_gather | solution.py:113
  128.7 4.1 copy-start.1
  128.7 4.1 copy-start.3
  134.4 82.5 %reduce-scatter.7.cloned.1.call-start = ((), (), s32[]{:S(2)}) async-start(), calls=%async_computation.7 | async-start | bytes 3145728 | tf_op jit(solution)/shard_map/reduce_scatter | solution.py:116
  167.6 11.5 %copy-start.20 = (bf16[2048,1024]{1,0:T(8,128)(2,1)S(1)}, bf16[2048,1024]{1,0:T(8,128)(2,1)}, u32[]{:S(2)}) copy-start(bf16[2048,1024]{1,0:T(8,128)(2,1)} %param.20) | copy-start | bytes 12582916
  177.1 2.0 copy-start.27
  184.8 35.2 %copy-start.13 = (f32[1024]{0:T(1024)S(1)}, f32[1024]{0:T(1024)}, u32[]{:S(2)}) copy-start(f32[1024]{0:T(1024)} %param.23) | copy-start | bytes 12292
  184.8 72.9 %all-gather.9.cloned.1.call-start = ((), (), s32[]{:S(2)}) async-start(), calls=%async_computation.8 | async-start | bytes 3145728 | tf_op jit(solution)/shard_map/all_gather | solution.py:128
  216.8 3.2 copy-start.8
  219.6 2.0 copy-start.19
  224.5 83.4 %reduce-scatter.9.cloned.1.call-start = ((), (), s32[]{:S(2)}) async-start(), calls=%async_computation.9 | async-start | bytes 3145728 | tf_op jit(solution)/shard_map/reduce_scatter | solution.py:133
  257.7 12.3 %copy-start.21 = (bf16[1024,2048]{1,0:T(8,128)(2,1)S(1)}, bf16[1024,2048]{1,0:T(8,128)(2,1)}, u32[]{:S(2)}) copy-start(bf16[1024,2048]{1,0:T(8,128)(2,1)} %param.19) | copy-start | bytes 12582916
  268.0 2.0 copy-start.25
  275.8 72.3 %all-gather.11.cloned.1.call-start = ((), (), s32[]{:S(2)}) async-start(), calls=%async_computation.10 | async-start | bytes 3145728 | tf_op jit(solution)/shard_map/all_gather | solution.py:144
  307.8 4.4 copy-start.2
  307.8 4.4 copy-start.4
  307.8 4.4 copy-start.5
  307.8 4.4 copy-start.9
  314.9 155.7 %reduce-scatter.11.cloned.1.call-start = ((), (), s32[]{:S(2)}) async-start(), calls=%async_computation.11 | async-start | bytes 3145728 | tf_op jit(solution)/shard_map/reduce_scatter | solution.py:183
  361.3 1.6 copy-start.6
  381.1 1.6 copy-start.6
  405.9 270.6 %all-reduce.4.cloned.1.call-start = ((), (), s32[]{:S(2)}) async-start(), calls=%async_computation.12 | async-start | bytes 25165824 | tf_op jit(solution)/shard_map/psum | solution.py:193
  406.1 9.6 %copy-start.24 = (bf16[1024,1024]{1,0:T(8,128)(2,1)S(1)}, bf16[1024,1024]{1,0:T(8,128)(2,1)}, u32[]{:S(2)}) copy-start(bf16[1024,1024]{1,0:T(8,128)(2,1)} %all-gather.7.cloned.1.call-done) | copy-start | bytes 6291460
  406.1 9.6 %copy-start.26 = (bf16[1024,2048]{1,0:T(8,128)(2,1)S(1)}, bf16[1024,2048]{1,0:T(8,128)(2,1)}, u32[]{:S(2)}) copy-start(bf16[1024,2048]{1,0:T(8,128)(2,1)} %copy-done.25) | copy-start | bytes 12582916
  415.7 6.3 copy-start.10
  415.7 6.3 copy-start.11
  415.7 8.5 %copy-start.23 = (bf16[1024,1024]{1,0:T(8,128)(2,1)S(1)}, bf16[1024,1024]{1,0:T(8,128)(2,1)}, u32[]{:S(2)}) copy-start(bf16[1024,1024]{1,0:T(8,128)(2,1)} %all-gather.5.cloned.1.call-done) | copy-start | bytes 6291460
  422.0 2.3 copy-start.22
  429.1 0.7 copy-start.14
  429.1 0.7 copy-start.15
  429.1 0.7 copy-start.17
  429.1 0.7 copy-start.18
  676.4 6.8 copy-start.7
Sparse Core Ops, SparseCore 0:
  9.5 35.8 all-gather.4
  96.8 31.8 reduce-scatter.4
  134.5 33.0 all-gather.6
  184.9 31.8 reduce-scatter.6
  224.6 33.0 all-gather.8
  275.9 31.8 reduce-scatter.8
  315.0 33.0 all-gather.10
  406.0 31.9 reduce-scatter.10
  443.1 233.2 all-reduce.3
where the time goes:
time: 711 us; the launch traced here: 703 us
  waiting for transfers between devices  435 us (61%)
  matrix products  102 us (14%)
  local copies, waits for them, and re-layouts  59.5 us (8%)
  other arithmetic  49.6 us (7%)
  blocking collectives  40.7 us (6%)
  between operations  14.3 us (2%)
    psum x1, waiting for transfers between devices, body(): lax.psum(grad_qkv_w.astype(jnp.bfloat16), 'dp').astype(jnp.float32)  203 us
    psum x1, blocking collectives, body(): lax.psum((grad_gain1, grad_bias1, grad_gain2, grad_bias2), ('dp', 'tensor'))  40.7 us
    all_gather x1, waiting for transfers between devices, body(): source = lax.all_gather(layer_input, 'tensor', axis=0, tiled=True)  36.6 us
    all_gather x1, waiting for transfers between devices, body(): attn_group = lax.all_gather(attn_low, 'tensor', axis=0, tiled=True)  33.2 us
    all_gather x1, waiting for transfers between devices, body(): hidden_group = lax.all_gather(hidden_low, 'tensor', axis=0, tiled=True)  33 us
    all_gather x1, waiting for transfers between devices, body(): branch_group = lax.all_gather(branch_low, 'tensor', axis=0, tiled=True)  33 us
    reduce_scatter x1, waiting for transfers between devices, body(): lax.psum_scatter(jnp.dot(attended, out_use, preferred_element_type=jnp.fl...  32 us
    reduce_scatter x1, waiting for transfers between devices, body(): lax.psum_scatter(contract_cols(grad_upper, w_up).astype(jnp.bfloat16), 't...  32 us
  transfers between devices with their start and end apart: 9, of which 8 were waited for; matrix products, arithmetic and copies ran while one was open for 4% of the time, Pallas kernels for 0%

commit v1 on v0

--- a/solution.py
+++ b/solution.py
@@ -9,6 +9,11 @@
 NEG_LARGE = -1e30
 SQRT_HALF = 0.7071067811865476
 INV_ROOT_TWO_PI = 0.3989422804014327
+
+
+def add_all(x, axis):
+    parts = lax.all_gather(x, axis)
+    return jnp.sum(parts, axis=0)
 
 
 def gelu_exact(values):
@@ -190,7 +195,7 @@
     ).astype(jnp.float32)
     grad_input = grad_first + input_part
     summed_qkv, summed_out, summed_up, summed_down = (
-        lax.psum(grad_qkv_w.astype(jnp.bfloat16), "dp").astype(jnp.float32),
+        add_all(grad_qkv_w.astype(jnp.bfloat16), "dp").astype(jnp.float32),
         lax.psum(grad_out_w.astype(jnp.bfloat16), "dp").astype(jnp.float32),
         lax.psum(grad_up.astype(jnp.bfloat16), "dp").astype(jnp.float32),
         lax.psum(grad_down.astype(jnp.bfloat16), "dp").astype(jnp.float32),

time: 711 us -> 967 us (1.36)
  waiting for transfers between devices: 435 us -> 617 us
  local copies, waits for them, and re-layouts: 59.5 us -> 104 us
  other arithmetic: 49.6 us -> 75.4 us
    all_gather x0 -> x1, waiting for transfers between devices: none -> 233 us  [add_all(): parts = lax.all_gather(x, axis)]
    psum x1, waiting for transfers between devices: 203 us -> 151 us  [body(): lax.psum(grad_out_w.astype(jnp.bfloat16), 'dp').astype(jnp.float32)]
    unnamed x55 -> x52, local copies, waits for them, and re-layouts: 10.2 us -> 54.8 us
    reduce_sum x0 -> x1, other arithmetic: none -> 24.6 us  [add_all(): return jnp.sum(parts, axis=0)]
  transfers between devices with their start and end apart: 9 -> 10, of which waited for: 8 -> 9; matrix products, arithmetic and copies ran while one was open for 4% -> 5% of each run, Pallas kernels for 0% -> 0%
where the time goes in v1:
time: 967 us; the launch traced here: 958 us
  waiting for transfers between devices  617 us (64%)
  matrix products  105 us (11%)
  local copies, waits for them, and re-layouts  104 us (11%)
  other arithmetic  75.4 us (8%)
  blocking collectives  41 us (4%)
  between operations  14.8 us (2%)
    all_gather x1, waiting for transfers between devices, add_all(): parts = lax.all_gather(x, axis)  233 us
    psum x1, waiting for transfers between devices, body(): lax.psum(grad_out_w.astype(jnp.bfloat16), 'dp').astype(jnp.float32)  151 us
    unnamed x52, local copies, waits for them, and re-layouts  54.8 us
    psum x1, blocking collectives, body(): lax.psum((grad_gain1, grad_bias1, grad_gain2, grad_bias2), ('dp', 'tensor'))  41 us
    all_gather x1, waiting for transfers between devices, body(): source = lax.all_gather(layer_input, 'tensor', axis=0, tiled=True)  36.6 us
    all_gather x1, waiting for transfers between devices, body(): attn_group = lax.all_gather(attn_low, 'tensor', axis=0, tiled=True)  33.2 us
    all_gather x1, waiting for transfers between devices, body(): hidden_group = lax.all_gather(hidden_low, 'tensor', axis=0, tiled=True)  33 us
    all_gather x1, waiting for transfers between devices, body(): branch_group = lax.all_gather(branch_low, 'tensor', axis=0, tiled=True)  32.8 us
  transfers between devices with their start and end apart: 10, of which 9 were waited for; matrix products, arithmetic and copies ran while one was open for 5% of the time, Pallas kernels for 0%

profile of v1, /device:TPU:0, one launch (start us, length us, event | category | flops | bytes accessed | tf_op | source)
XLA Modules:
  0.0 958.3 jit_solution(9449035254353323641)
XLA Ops:
  8.8 36.6 %all-gather.7.cloned.1.call-done = bf16[1024,1024]{1,0:T(8,128)(2,1)} async-done(((bf16[512,1024]{1,0:T(8,128)(2,1)}), bf16[1024,1024]{1,0:T(8,128)(2,1)}) %all-gather.7.cloned.1.call-update) | async-done | bytes 2097168 | tf_op jit(solution)/shard_map/all_gather | solution.py:82
  45.4 6.3 convolution_convert_fusion.2
  51.7 8.9 reshape.243
  60.6 7.6 copy.46
  68.2 24.2 %while.22 = (s32[]{:T(128)}, bf16[2,512,512]{2,1,0:T(8,128)(2,1)}, f32[2,8,512]{2,1,0:T(8,128)S(1)}, bf16[2,512,3,8,64]{1,4,3,2,0:T(8,128)(2,1)}, s32[2,512]{1,0:T(2,128)S(1)}, /*index=5*/s32[]{:T(128)}) while((s32[]{:T(128)}, bf16[2,512,512]{2,1,0:T(8,128)(2,1)}, f32[2,8,512]{2,1,0:T(8,128)S(1)}, bf16[2,512,3,8,64]{1,4,3,2,0:T(8,128)(2,1)}, ...), condition=%wide.region_3.4_spmd, body=%wide.region_0.3_spmd.sunk | while | flops 562556928 | bytes 33691740 | solution.py:106
  68.5 1.5 dynamic-slice_bitcast_fusion.6
  71.5 1.7 fusion.86
  73.2 3.2 fusion.87
  76.4 2.0 copy.72
  78.5 1.9 constant_dynamic-update-slice_fusion.4
  80.6 1.5 dynamic-slice_bitcast_fusion.6
  83.6 1.7 fusion.86
  85.3 3.2 fusion.87
  88.6 2.0 copy.72
  90.6 1.9 constant_dynamic-update-slice_fusion.4
  92.5 4.1 convolution_convert_fusion.5
  96.7 32.0 %reduce-scatter.5.cloned.1.call-done = bf16[512,1024]{1,0:T(8,128)(2,1)} async-done(((bf16[1024,1024]{1,0:T(8,128)(2,1)}), bf16[512,1024]{1,0:T(8,128)(2,1)}) %reduce-scatter.5.cloned.1.call-update) | async-done | bytes 1048592 | tf_op jit(solution)/shard_map/reduce_scatter | solution.py:108
  128.7 2.0 fusion.42
  130.7 2.0 multiply_reduce_fusion.4
  134.6 33.0 %all-gather.9.cloned.1.call-done = bf16[1024,1024]{1,0:T(8,128)(2,1)} async-done(((bf16[512,1024]{1,0:T(8,128)(2,1)}), bf16[1024,1024]{1,0:T(8,128)(2,1)}) %all-gather.9.cloned.1.call-update) | async-done | bytes 2097168 | tf_op jit(solution)/shard_map/all_gather | solution.py:118
  167.6 9.5 multiply_convert_fusion.1
  177.1 2.0 copy-done.25
  179.1 5.7 convolution_convert_fusion.4
  184.8 32.0 %reduce-scatter.7.cloned.1.call-done = bf16[512,1024]{1,0:T(8,128)(2,1)} async-done(((bf16[1024,1024]{1,0:T(8,128)(2,1)}), bf16[512,1024]{1,0:T(8,128)(2,1)}) %reduce-scatter.7.cloned.1.call-update) | async-done | bytes 1048592 | tf_op jit(solution)/shard_map/reduce_scatter | solution.py:121
  216.8 2.8 fusion.49
  220.0 1.6 fusion.38
  221.6 2.9 fusion.47
  224.9 32.8 %all-gather.11.cloned.1.call-done = bf16[1024,1024]{1,0:T(8,128)(2,1)} async-done(((bf16[512,1024]{1,0:T(8,128)(2,1)}), bf16[1024,1024]{1,0:T(8,128)(2,1)}) %all-gather.11.cloned.1.call-update) | async-done | bytes 2097168 | tf_op jit(solution)/shard_map/all_gather | solution.py:133
  257.7 10.3 %fusion.31 = bf16[1024,2048]{1,0:T(8,128)(2,1)S(1)} fusion(f32[1024,2048]{1,0:T(8,128)} %get-tuple-element.165, bf16[1024,1024]{1,0:T(8,128)(2,1)} %all-gather.11.cloned.1.call-done, bf16[2048,1024]{1,0:T(8,128)(2,1)} %param.20), kind=kOutput, calls=%fused_computation.54 | convolution fusion | flops 4315938816 | bytes 18874368 | tf_op jit(solution)/shard_map/dot_general | solution.py:60
  268.0 2.0 copy-done.23
  270.0 5.7 convolution_convert_fusion.3
  275.8 32.0 %reduce-scatter.9.cloned.1.call-done = bf16[512,1024]{1,0:T(8,128)(2,1)} async-done(((bf16[1024,1024]{1,0:T(8,128)(2,1)}), bf16[512,1024]{1,0:T(8,128)(2,1)}) %reduce-scatter.9.cloned.1.call-update) | async-done | bytes 1048592 | tf_op jit(solution)/shard_map/reduce_scatter | solution.py:138
  307.8 4.4 multiply_reduce_fusion.1
  312.3 2.5 fusion.46
  314.9 33.2 %all-gather.13.cloned.1.call-done = bf16[1024,1024]{1,0:T(8,128)(2,1)} async-done(((bf16[512,1024]{1,0:T(8,128)(2,1)}), bf16[1024,1024]{1,0:T(8,128)(2,1)}) %all-gather.13.cloned.1.call-update) | async-done | bytes 2097168 | tf_op jit(solution)/shard_map/all_gather | solution.py:149
  348.1 4.1 convolution_convert_fusion.7
  352.2 4.0 reshape.242
  356.3 3.3 copy.50
  359.6 39.5 %while.23 = (s32[]{:T(128)}, bf16[2,512,3,512]{3,1,0,2:T(8,128)(2,1)}, bf16[2,512,3,8,64]{1,4,3,2,0:T(8,128)(2,1)}, s32[2,512]{1,0:T(2,128)S(1)}, f32[2,8,512]{2...) while((s32[]{:T(128)}, bf16[2,512,3,512]{3,1,0,2:T(8,128)(2,1)}, ...), condition=%wide.region_17.18_spmd, body=%wide.region_15.17_spmd.sunk | while | flops 1376776192 | bytes 86104192 | solution.py:183
  362.6 2.3 fusion.93
  364.9 2.9 multiply_reduce_fusion.7
  367.9 2.7 multiply_convert_fusion.3
  374.0 2.6 copy.73
  376.6 2.7 constant_dynamic-update-slice_fusion.5
  382.4 2.3 fusion.93
  384.7 2.9 multiply_reduce_fusion.7
  387.6 2.7 multiply_convert_fusion.3
  393.8 2.6 copy.73
  396.4 2.6 constant_dynamic-update-slice_fusion.5
  399.0 6.6 bitcast_convert_fusion
  405.9 9.6 %convolution_convert_fusion = bf16[2048,1024]{1,0:T(8,128)(2,1)} fusion(bf16[1024,2048]{1,0:T(8,128)(2,1)} %copy-done.25, bf16[1024,1024]{1,0:T(8,128)(2,1)} %all-gather.11.cloned.1.call-done), kind=kOutput, calls=%fused_computation.58 | convolution fusion | flops 4297064448 | bytes 10485760 | tf_op jit(solution)/shard_map/dot_general | solution.py:54
  415.5 6.2 convolution_convert_fusion.1
  421.7 2.2 convolution_convert_fusion.6
  424.0 7.7 convert_bitcast_fusion
  432.5 41.0 %all-reduce = (f32[1024]{0:T(1024)}, f32[1024]{0:T(1024)}, f32[1024]{0:T(1024)}, f32[1024]{0:T(1024)}) all-reduce(f32[1024]{0:T(1024)S(1)} %copy-done.17, f32[1024]{0:T(1024)S(1)} %copy-done.18, f32[1024]{0:T(1024)S(1)} %copy-done.14, f32[1024]{0:T(1024)S(1)} %copy-done.15), channel_id=1, replica_groups=mesh['dp'=16,'tensor'=2] {'dp','tensor'}, use_global_device_ids=true, to_apply=%region_24.25 | all-reduce | flops 4096 | bytes 32768 | tf_op jit(solution)/shard_map/psum | solution.py:203
  473.5 3.2 add_convert_fusion
  476.7 151.2 %all-reduce.4.cloned.1.call-done = (bf16[512,1024]{1,0:T(8,128)(2,1)}, bf16[1024,2048]{1,0:T(8,128)(2,1)}, bf16[2048,1024]{1,0:T(8,128)(2,1)}) async-done(((bf16[512,1024]{1,0:T(8,128)(2,1)}, bf16[1024,2048]{1,0:T(8,128)(2,1)}, bf16[2048,1024]{1,0:T(8,128)(2,1)}), (bf16[512,1024]{1,0:T(8,128)(2,1)}, bf16[1024,2048]{1,0:T(8,128)(2,1)}, bf16[2048,1024]{1,0:T(8,128)(2,1)})) %all-reduce.4.cloned.1.call-update) | async-done | bytes 9437200 | tf_op jit(solution)/shard_map/psum | solution.py:199
  627.9 2.8 convert_element_type.142
  630.7 8.0 convert_element_type.144
  638.7 4.4 convert_element_type.146
  643.1 233.3 %all-gather.15.cloned.1.call-done = bf16[16384,3,512]{0,2,1:T(8,128)(2,1)} async-done(((bf16[1024,3,512]{0,2,1:T(8,128)(2,1)}), bf16[16384,3,512]{0,2,1:T(8,128)(2,1)}) %all-gather.15.cloned.1.call-update) | async-done | bytes 50331664 | tf_op jit(solution)/shard_map/all_gather | solution.py:15
  876.5 44.6 %copy.68 = bf16[192,8,16,1024]{3,2,1,0:T(8,128)(2,1)} copy(bf16[192,8,16,1024]{3,1,2,0:T(8,128)(2,1)} %bitcast.145) | data formatting | bytes 100663296
  921.1 24.6 %reduce_sum.146 = bf16[1024,3,512]{0,2,1:T(8,128)(2,1)} reduce(bf16[16,1024,3,512]{1,0,3,2:T(8,128)(2,1)} %bitcast.142, bf16[]{:T(256)} %constant.63.clone.1), dimensions={0}, to_apply=%region_19.20 | reduce | flops 23592960 | bytes 53477376 | tf_op jit(solution)/shard_map/reduce_sum | solution.py:16
  945.6 5.4 copy.53
  (110 shorter events, 22.1 us)
Async XLA Ops:
  7.2 38.2 %copy-start = (bf16[1024,3,512]{2,0,1:T(8,128)(2,1)S(1)}, bf16[1024,3,512]{2,0,1:T(8,128)(2,1)}, u32[]{:S(2)}) copy-start(bf16[1024,3,512]{2,0,1:T(8,128)(2,1)} %param.17) | copy-start | bytes 9437188
  7.2 38.2 %all-gather.7.cloned.1.call-start = ((), (), s32[]{:S(2)}) async-start(), calls=%async_computation.4 | async-start | bytes 3145728 | tf_op jit(solution)/shard_map/all_gather | solution.py:82
  7.9 120.8 %reduce-scatter.5.cloned.1.call-start = ((), (), s32[]{:S(2)}) async-start(), calls=%async_computation.5 | async-start | bytes 3145728 | tf_op jit(solution)/shard_map/reduce_scatter | solution.py:108
  96.6 36.2 %copy-start.12 = (f32[1024]{0:T(1024)S(1)}, f32[1024]{0:T(1024)}, u32[]{:S(2)}) copy-start(f32[1024]{0:T(1024)} %param.21) | copy-start | bytes 12292
  96.6 36.2 %copy-start.16 = (f32[1024]{0:T(1024)S(1)}, f32[1024]{0:T(1024)}, u32[]{:S(2)}) copy-start(f32[1024]{0:T(1024)} %param.22) | copy-start | bytes 12292
  96.6 71.0 %all-gather.9.cloned.1.call-start = ((), (), s32[]{:S(2)}) async-start(), calls=%async_computation.6 | async-start | bytes 3145728 | tf_op jit(solution)/shard_map/all_gather | solution.py:118
  128.7 4.1 copy-start.1
  128.7 4.1 copy-start.3
  134.3 82.5 %reduce-scatter.7.cloned.1.call-start = ((), (), s32[]{:S(2)}) async-start(), calls=%async_computation.7 | async-start | bytes 3145728 | tf_op jit(solution)/shard_map/reduce_scatter | solution.py:121
  167.6 11.5 %copy-start.20 = (bf16[2048,1024]{1,0:T(8,128)(2,1)S(1)}, bf16[2048,1024]{1,0:T(8,128)(2,1)}, u32[]{:S(2)}) copy-start(bf16[2048,1024]{1,0:T(8,128)(2,1)} %param.20) | copy-start | bytes 12582916
  177.1 2.0 copy-start.25
  184.7 35.2 %copy-start.13 = (f32[1024]{0:T(1024)S(1)}, f32[1024]{0:T(1024)}, u32[]{:S(2)}) copy-start(f32[1024]{0:T(1024)} %param.23) | copy-start | bytes 12292
  184.8 72.9 %all-gather.11.cloned.1.call-start = ((), (), s32[]{:S(2)}) async-start(), calls=%async_computation.8 | async-start | bytes 3145728 | tf_op jit(solution)/shard_map/all_gather | solution.py:133
  216.8 3.2 copy-start.8
  219.6 2.0 copy-start.19
  224.4 83.4 %reduce-scatter.9.cloned.1.call-start = ((), (), s32[]{:S(2)}) async-start(), calls=%async_computation.9 | async-start | bytes 3145728 | tf_op jit(solution)/shard_map/reduce_scatter | solution.py:138
  257.7 12.3 %copy-start.21 = (bf16[1024,2048]{1,0:T(8,128)(2,1)S(1)}, bf16[1024,2048]{1,0:T(8,128)(2,1)}, u32[]{:S(2)}) copy-start(bf16[1024,2048]{1,0:T(8,128)(2,1)} %param.19) | copy-start | bytes 12582916
  268.0 2.0 copy-start.23
  275.7 72.4 %all-gather.13.cloned.1.call-start = ((), (), s32[]{:S(2)}) async-start(), calls=%async_computation.10 | async-start | bytes 3145728 | tf_op jit(solution)/shard_map/all_gather | solution.py:149
  307.8 4.4 copy-start.2
  307.8 4.4 copy-start.4
  307.8 4.4 copy-start.5
  307.8 4.4 copy-start.9
  314.8 158.7 %reduce-scatter.11.cloned.1.call-start = ((), (), s32[]{:S(2)}) async-start(), calls=%async_computation.11 | async-start | bytes 3145728 | tf_op jit(solution)/shard_map/reduce_scatter | solution.py:188
  361.3 1.3 copy-start.6
  381.1 1.3 copy-start.6
  405.6 222.3 %all-reduce.4.cloned.1.call-start = ((), (), s32[]{:S(2)}) async-start(), calls=%async_computation.13 | async-start | bytes 18874368 | tf_op jit(solution)/shard_map/psum | solution.py:199
  405.9 9.6 %copy-start.22 = (bf16[1024,1024]{1,0:T(8,128)(2,1)S(1)}, bf16[1024,1024]{1,0:T(8,128)(2,1)}, u32[]{:S(2)}) copy-start(bf16[1024,1024]{1,0:T(8,128)(2,1)} %all-gather.9.cloned.1.call-done) | copy-start | bytes 6291460
  405.9 9.6 %copy-start.24 = (bf16[1024,2048]{1,0:T(8,128)(2,1)S(1)}, bf16[1024,2048]{1,0:T(8,128)(2,1)}, u32[]{:S(2)}) copy-start(bf16[1024,2048]{1,0:T(8,128)(2,1)} %copy-done.23) | copy-start | bytes 12582916
  415.5 6.3 copy-start.10
  415.5 6.3 copy-start.11
  424.0 452.5 %all-gather.15.cloned.1.call-start = ((), (), s32[]{:S(2)}) async-start(), calls=%async_computation.12 | async-start | bytes 53477376 | tf_op jit(solution)/shard_map/all_gather | solution.py:15
  431.7 0.7 copy-start.14
  431.7 0.7 copy-start.15
  431.7 0.7 copy-start.17
  431.7 0.7 copy-start.18
  630.7 8.0 copy-start.7
Sparse Core Ops, SparseCore 0:
  9.5 35.8 all-gather.6
  96.7 31.8 reduce-scatter.4
  134.5 33.0 all-gather.8
  184.9 31.8 reduce-scatter.6
  224.6 33.0 all-gather.10
  275.8 31.9 reduce-scatter.8
  315.0 33.0 all-gather.12
  405.7 31.8 reduce-scatter.10
  442.2 185.5 all-reduce.3
  629.3 247.1 all-gather.14
